TPU v7x, 32 devices: a whole 2x2x4 slice. The times are simulated.
32 devices in a mesh: gz: 16 (over z, y, core), gy: 2 (over x).
Axes of the slice: x: 2, y: 2, z: 4, core: 2. Of those that a mesh axis runs over, the one named last changes fastest.
Arguments:
- estimate: float32 [256, 64, 512], P('gz', 'gy'), may hold values from 0.5 to 2
- measured: float32 [4, 256, 64, 512], P(None, 'gz', 'gy'), may hold values from 0.25 to 4
- psf_z: float32 [4, 31], replicated, may hold values from 0.1 to 1
- psf_y: float32 [4, 15], replicated, may hold values from 0.1 to 1
- psf_x: float32 [4, 15], replicated, may hold values from 0.1 to 1
- extents: int32 [4, 3], replicated, may hold values from 9 to 31, as said below
- order: int32 [4], replicated, may hold values from 0 to 3, each once
Outputs:
- updated: float32 [256, 64, 512], P('gz', 'gy')
Inputs may be any that keep to these rules, and one draw needn't show every extreme that they name: `extents`: every extent is odd; along z it lies in 9 to 31, along y and x in 9 to 15; in every draw some view has extent 31 along z and some view has extent 15 along y.
All inputs are finite; a program needn't handle non-finite values.
Results may differ from a plain program's by a relative error of at most 0.0001.
Values sent between devices are 32-bit elements; how exact they have to be, the bound alone decides.
A program may use at most 64 MiB of HBM per device.

v0:
```python
import functools
import jax
import jax.numpy as jnp
from jax import lax
from jax.experimental import pallas as pl
from jax.experimental.pallas import tpu as pltpu
from jax.sharding import PartitionSpec as P

MESH = pl.DeviceIdType.MESH
RZ = 15
RL = 7
LANES = 128


def with_halo(value, sides, width):
    for axis, dim in sides:
        size, length = (lax.axis_size(axis), value.shape[dim])
        up = [(i, (i + 1) % size) for i in range(size - 1)]
        down = [(j, i) for i, j in up]
        last = lax.slice_in_dim(value, length - width, length, axis=dim)
        initial = lax.slice_in_dim(value, 0, width, axis=dim)
        before = lax.ppermute(last, axis, up)
        after = lax.ppermute(initial, axis, down)
        value = jnp.concatenate([before, value, after], axis=dim)
    return value


def line_taps(profile, reach_cells, tap_reach):
    offsets = jnp.arange(2 * tap_reach + 1, dtype=jnp.int32) - tap_reach
    kept = jnp.where(jnp.abs(offsets) <= reach_cells, profile, jnp.zeros_like(profile))
    return kept / jnp.sum(kept)


def correlate_padded(padded, weights, along_axis, tap_reach, length, flipped):
    total = None
    for offset in range(2 * tap_reach + 1):
        start = 2 * tap_reach - offset if flipped else offset
        piece = lax.slice_in_dim(padded, start, start + length, axis=along_axis)
        term = weights[offset] * piece
        total = term if total is None else total + term
    return total


def blur(field, weights_z, weights_y, weights_x, flipped):
    padded = with_halo(field, (("gz", 0),), RZ)
    result = correlate_padded(padded, weights_z, 0, RZ, field.shape[0], flipped)
    widened = with_halo(result, (("gy", 1),), RL)
    result = correlate_padded(widened, weights_y, 1, RL, field.shape[1], flipped)
    result = jnp.pad(result, ((0, 0), (0, 0), (RL, RL)))
    return correlate_padded(result, weights_x, 2, RL, field.shape[2], flipped)


def general(estimate, measured, psf_z, psf_y, psf_x, extents, order):
    current = estimate
    for position in range(measured.shape[0]):
        view = order[position]
        radii = (extents[view] - 1) // 2
        weights_z = line_taps(psf_z[view], radii[0], RZ)
        weights_y = line_taps(psf_y[view], radii[1], RL)
        weights_x = line_taps(psf_x[view], radii[2], RL)
        recorded = lax.dynamic_index_in_dim(measured, view, 0, keepdims=False)
        blurred = blur(current, weights_z, weights_y, weights_x, False)
        ratio = recorded / blurred
        current = current * blur(ratio, weights_z, weights_y, weights_x, True)
    return current


def place():
    g = lax.axis_index("gz")
    w = lax.axis_index("gy")
    return g // 4, (g // 2) % 2, g % 2, w


def slab_of(a, w):
    return 2 * a + lax.rem(w + a, 2)


def group_peers():
    h, a, c, w = place()
    peers = []
    for k in range(1, 8):
        da, dc, dw = k // 4, (k // 2) % 2, k % 2
        device = (4 * h + 2 * lax.rem(a + da, 2) + lax.rem(c + dc, 2), lax.rem(w + dw, 2))
        peers.append(device)
    return peers


def spread_kernel(nz, ny, back, srcs, dst_ref, send, recv, local, between=None):
    h, a, c, w = place()
    barrier = pltpu.get_barrier_semaphore()
    for device in group_peers():
        pl.semaphore_signal(barrier, inc=1, device_id=device, device_id_type=MESH)
    pl.semaphore_wait(barrier, 7)
    for phase in ("start", "wait"):
        for k in range(4):
            da, dw = k // 2, k % 2
            if not back:
                ta, tw = lax.rem(c + da, 2), lax.rem(w + dw, 2)
                device = (4 * h + 2 * ta + a, tw)
                x0 = pl.multiple_of(LANES * slab_of(ta, tw), LANES)
                src = srcs.at[:, :, pl.ds(x0, LANES)]
                dst = dst_ref.at[pl.ds(nz * c, nz), pl.ds(pl.multiple_of(ny * w, 8), ny), :]
            else:
                tc, tw = lax.rem(a + da, 2), lax.rem(w + dw, 2)
                device = (4 * h + 2 * c + tc, tw)
                x0 = pl.multiple_of(LANES * slab_of(a, w), LANES)
                src = srcs.at[pl.ds(nz * tc, nz), pl.ds(pl.multiple_of(ny * tw, 8), ny), :]
                dst = dst_ref.at[:, :, pl.ds(x0, LANES)]
            remote = pltpu.make_async_remote_copy(
                src_ref=src, dst_ref=dst, send_sem=send.at[k], recv_sem=recv.at[k],
                device_id=device, device_id_type=MESH)
            if k:
                if phase == "start":
                    remote.start()
                else:
                    remote.wait()
                continue
            here = pltpu.make_async_copy(src, dst, local)
            if phase == "start":
                @pl.when(c == a)
                def _():
                    here.start()

                @pl.when(c != a)
                def _():
                    remote.start()
            else:
                @pl.when(c == a)
                def _():
                    here.wait()

                @pl.when(c != a)
                def _():
                    remote.wait()
        if phase == "start" and between is not None:
            between()


SPREAD_SEMS = [
    pltpu.SemaphoreType.DMA((4,)),
    pltpu.SemaphoreType.DMA((4,)),
    pltpu.SemaphoreType.DMA,
]


def back_kernel(nz, ny, src, dst, send, recv, local):
    spread_kernel(nz, ny, True, src, dst, send, recv, local)


def gather_back(current, nz, ny, nx):
    return pl.pallas_call(
        functools.partial(back_kernel, nz, ny),
        out_shape=jax.ShapeDtypeStruct((nz, ny, nx), jnp.float32),
        in_specs=[pl.BlockSpec(memory_space=pl.ANY)],
        out_specs=pl.BlockSpec(memory_space=pl.ANY),
        scratch_shapes=SPREAD_SEMS,
        compiler_params=pltpu.CompilerParams(collective_id=2, has_side_effects=True),
    )(current)


def taps_of(profile, view, radius, reach):
    kept = []
    for k in range(2 * reach + 1):
        value = jnp.full((8, LANES), profile[view, k], jnp.float32)
        kept.append(jnp.where(abs(k - reach) <= radius, value, jnp.zeros_like(value)))
    total = kept[0]
    for value in kept[1:]:
        total = total + value
    return [value / total for value in kept]


def band(taps, which):
    total = jnp.zeros(which.shape, jnp.float32)
    for k, tap in enumerate(taps):
        total = jnp.where(which == k, tap[0:1, :], total)
    return split(total)


def first_kernel(nz, ny, views, est, psf_z, psf_y, psf_x, extents, order, *refs):
    n = 2 * views
    dst, wz, ym, xm, xe = refs[0], refs[1:1 + n], refs[1 + n:1 + 2 * n], refs[1 + 2 * n:1 + 3 * n], refs[1 + 3 * n:1 + 4 * n]
    send, recv, local = refs[1 + 4 * n:]
    rows = 2 * ny

    def build():
        def iota(shape, dim):
            return lax.broadcasted_iota(jnp.int32, shape, dim)

        y_which = lax.rem(iota((rows, LANES), 1), rows) - iota((rows, LANES), 0) + RL
        x_which = iota((LANES, LANES), 0) - iota((LANES, LANES), 1) + RL
        r = iota((16, LANES), 0)
        e_which = jnp.where(r < 8, r - 8, r + (LANES - 8)) - iota((16, LANES), 1) + RL
        for p in range(views):
            view = order[p]
            tz = taps_of(psf_z, view, (extents[view, 0] - 1) // 2, RZ)
            ty = taps_of(psf_y, view, (extents[view, 1] - 1) // 2, RL)
            tx = taps_of(psf_x, view, (extents[view, 2] - 1) // 2, RL)
            for i in (2 * p, 2 * p + 1):
                for k in range(2 * RZ + 1):
                    wz[i][k] = tz[k]
                hi, lo = band(ty, y_which)
                ym[i][:, :LANES] = hi
                ym[i][:, LANES:] = lo
                hi, lo = band(tx, x_which)
                for top in (0, LANES):
                    xm[i][top:top + LANES, :LANES] = hi
                    xm[i][top:top + LANES, LANES:] = lo
                hi, lo = band(tx, e_which)
                xe[i][...] = jnp.zeros_like(xe[i])
                for top in (0, LANES):
                    xe[i][top:top + 16, :LANES] = hi
                    xe[i][top:top + 16, LANES:] = lo
                tz, ty, tx = tz[::-1], ty[::-1], tx[::-1]

    spread_kernel(nz, ny, False, est, dst, send, recv, local, build)


def spread_first(estimate, psf_z, psf_y, psf_x, extents, order):
    nz, ny, nx = estimate.shape
    views = order.shape[0]
    n = 2 * views
    smem = pl.BlockSpec(memory_space=pltpu.SMEM)
    vmem = pl.BlockSpec(memory_space=pltpu.VMEM)
    like = jax.ShapeDtypeStruct
    out = pl.pallas_call(
        functools.partial(first_kernel, nz, ny, views),
        out_shape=[like((2 * nz, 2 * ny, LANES), jnp.float32)]
        + [like((2 * RZ + 1, 8, LANES), jnp.float32)] * n
        + [like((2 * ny, 2 * LANES), jnp.bfloat16)] * n
        + [like((2 * LANES, 2 * LANES), jnp.bfloat16)] * (2 * n),
        in_specs=[pl.BlockSpec(memory_space=pl.ANY)] + [smem] * 5,
        out_specs=[pl.BlockSpec(memory_space=pl.ANY)] + [vmem] * (4 * n),
        scratch_shapes=SPREAD_SEMS,
        compiler_params=pltpu.CompilerParams(collective_id=1, has_side_effects=True),
    )(estimate, psf_z, psf_y, psf_x, extents, order)
    return out[0], [out[1 + i::n][:4] for i in range(n)]


def split(value):
    hi = value.astype(jnp.bfloat16)
    lo = (value - hi.astype(jnp.float32)).astype(jnp.bfloat16)
    return hi, lo


CHUNKS = 4


def blur_kernel(kind, chain, *refs):
    divide = kind in (0, 2)
    refs = list(refs)
    f = refs.pop(0)
    other = refs.pop(0) if kind else None
    wz, ym, xm, xe = [refs.pop(0) for _ in range(4)]
    if kind < 3:
        view, measured = refs.pop(0), refs.pop(0)
    out = refs.pop(0)
    if kind == 1:
        moved = refs.pop(0)
    below, above, zb, pack_l, pack_r, got_l, got_r, zs, zr, xs, xr = refs[:11]
    refs = refs[11:]
    if kind < 3:
        stage, chosen, bs, br, bl = refs[:5]
        if kind != 1:
            moved = refs[5]
        nb = chosen.shape[0]
        ny = chosen.shape[1]
        nz = measured.shape[1]
    planes, rows, _ = f.shape
    h, a, c, w = place()
    zi = 2 * h + c
    s = slab_of(a, w)
    has_dn, has_up = zi > 0, zi < chain - 1
    has_l, has_r = s > 0, s < 3

    def z_dev(i):
        return (4 * (i // 2) + 2 * a + lax.rem(i, 2), w)

    def x_dev(i):
        b = i // 2
        return (4 * h + 2 * b + c, lax.rem(i + b, 2))

    up, dn = z_dev(lax.rem(zi + 1, chain)), z_dev(lax.rem(zi + chain - 1, chain))
    lf, rt = x_dev(lax.rem(s + 3, 4)), x_dev(lax.rem(s + 1, 4))

    barrier = pltpu.get_barrier_semaphore()
    greet = [(has_up, up), (has_dn, dn), (has_l, lf), (has_r, rt)]
    for there, device in greet:
        @pl.when(there)
        def _():
            pl.semaphore_signal(barrier, inc=1, device_id=device, device_id_type=MESH)
    peers = sum(there.astype(jnp.int32) for there, _ in greet)
    if kind < 3:
        for k in range(4):
            device = (4 * h + 2 * c + lax.rem(a + k // 2, 2), lax.rem(w + k % 2, 2))
            if k:
                pl.semaphore_signal(barrier, inc=1, device_id=device, device_id_type=MESH)
            else:
                @pl.when(c != a)
                def _():
                    pl.semaphore_signal(barrier, inc=1, device_id=device, device_id_type=MESH)
        peers = peers + 3 + (c != a).astype(jnp.int32)
        start = nz // 2 if kind == 2 else 0
        fetch = pltpu.make_async_copy(measured.at[:, pl.ds(start, nb)], stage, bl)
        fetch.start()
    pl.semaphore_wait(barrier, peers)

    part = rows // CHUNKS

    def z_copy(side, j):
        ys = pl.ds(j * part, part)
        if side == 0:
            return pltpu.make_async_remote_copy(
                src_ref=f.at[pl.ds(planes - RZ, RZ), ys, :], dst_ref=below.at[:, ys, :],
                send_sem=zs.at[0, j], recv_sem=zr.at[0, j], device_id=up, device_id_type=MESH)
        return pltpu.make_async_remote_copy(
            src_ref=f.at[pl.ds(0, RZ), ys, :], dst_ref=above.at[:, ys, :],
            send_sem=zs.at[1, j], recv_sem=zr.at[1, j], device_id=dn, device_id_type=MESH)

    def x_copy(side):
        if side == 0:
            return pltpu.make_async_remote_copy(
                src_ref=pack_r, dst_ref=got_l,
                send_sem=xs.at[0], recv_sem=xr.at[0], device_id=rt, device_id_type=MESH)
        return pltpu.make_async_remote_copy(
            src_ref=pack_l, dst_ref=got_r,
            send_sem=xs.at[1], recv_sem=xr.at[1], device_id=lf, device_id_type=MESH)

    for j in range(CHUNKS):
        @pl.when(has_up)
        def _():
            z_copy(0, j).start()

        @pl.when(has_dn)
        def _():
            z_copy(1, j).start()

    def bulk(k):
        da, dw = k // 2, k % 2
        ta, tw = lax.rem(c + da, 2), lax.rem(w + dw, 2)
        x0 = pl.multiple_of(LANES * slab_of(ta, tw), LANES)
        return pltpu.make_async_remote_copy(
            src_ref=chosen.at[:, :, pl.ds(x0, LANES)],
            dst_ref=moved.at[pl.ds(nb * c, nb), pl.ds(pl.multiple_of(ny * w, 8), ny), :],
            send_sem=bs.at[k], recv_sem=br.at[k],
            device_id=(4 * h + 2 * ta + a, tw), device_id_type=MESH)

    def bulk_wait():
        for k in range(4):
            if k:
                bulk(k).wait()
            else:
                @pl.when(c != a)
                def _():
                    bulk(0).wait()

    if kind < 3:
        fetch.wait()
        chosen[...] = stage[view[0]]

        @pl.when(c != a)
        def _():
            bulk(0).start()

        for k in range(1, 4):
            bulk(k).start()

        @pl.when(c == a)
        def _():
            x0 = pl.multiple_of(LANES * slab_of(c, w), LANES)
            moved[pl.ds(nb * c, nb), pl.ds(pl.multiple_of(ny * w, 8), ny), :] = chosen[:, :, pl.ds(x0, LANES)]

    @pl.when(jnp.logical_not(has_dn))
    def _():
        below[...] = jnp.zeros_like(below)

    @pl.when(jnp.logical_not(has_up))
    def _():
        above[...] = jnp.zeros_like(above)

    @pl.when(jnp.logical_not(has_l))
    def _():
        got_l[...] = jnp.zeros_like(got_l)

    @pl.when(jnp.logical_not(has_r))
    def _():
        got_r[...] = jnp.zeros_like(got_r)

    half = 16

    def z_tile(t, carry):
        ys = pl.ds(pl.multiple_of(8 * t, 8), 8)
        taps = [wz[k] for k in range(2 * RZ + 1)]
        for first in range(0, planes, half):
            acc = [None] * half
            for p in range(first, first + half + 2 * RZ):
                if p < RZ:
                    v = below[p, ys, :]
                elif p < RZ + planes:
                    v = f[p - RZ, ys, :]
                else:
                    v = above[p - RZ - planes, ys, :]
                for o in range(half):
                    k = p - first - o
                    if 0 <= k <= 2 * RZ:
                        term = taps[k] * v
                        acc[o] = term if acc[o] is None else acc[o] + term
            for o in range(half):
                zb[first + o, ys, :] = acc[o]
        return carry

    for j in range(CHUNKS):
        @pl.when(has_dn)
        def _():
            z_copy(0, j).wait_recv()

        @pl.when(has_up)
        def _():
            z_copy(1, j).wait_recv()

        lax.fori_loop(j * part // 8, (j + 1) * part // 8, z_tile, 0)

    for j in range(CHUNKS):
        @pl.when(has_up)
        def _():
            z_copy(0, j).wait_send()

        @pl.when(has_dn)
        def _():
            z_copy(1, j).wait_send()

    lane = lax.broadcasted_iota(jnp.int32, (rows, LANES), 1)
    per = LANES // 8

    for q in range(planes // per):
        packed_l = packed_r = None
        for k in range(0, per, 2):
            p = q * per + k
            his, los = zip(*(split(zb[p + i]) for i in range(2)))
            hi = jnp.concatenate(his, axis=1)
            lo = jnp.concatenate(los, axis=1)
            got = jnp.dot(ym[...], jnp.concatenate([hi, lo, hi, lo], axis=0),
                          preferred_element_type=jnp.float32)
            for i in range(2):
                value = got[:, i * LANES:(i + 1) * LANES]
                zb[p + i] = value
                at = 8 * (k + i)
                left = value if at == 0 else pltpu.roll(value, at, 1)
                right = pltpu.roll(value, (at + 8) % LANES, 1) if at + 8 < LANES else value
                if packed_l is None:
                    packed_l, packed_r = left, right
                else:
                    packed_l = jnp.where(lane >= at, left, packed_l)
                    packed_r = jnp.where(lane >= at, right, packed_r)
        pack_l[q] = packed_l
        pack_r[q] = packed_r

    @pl.when(has_r)
    def _():
        x_copy(0).start()

    @pl.when(has_l)
    def _():
        x_copy(1).start()

    step = 4
    for p in range(0, planes, step):
        hi, lo = split(zb[p:p + step].reshape(step * rows, LANES))
        got = jnp.dot(jnp.concatenate([hi, lo], axis=1), xm[...], preferred_element_type=jnp.float32)
        zb[p:p + step] = (got[:, :LANES] + got[:, LANES:]).reshape(step, rows, LANES)

    @pl.when(has_l)
    def _():
        x_copy(0).wait_recv()

    @pl.when(has_r)
    def _():
        x_copy(1).wait_recv()

    if divide:
        bulk_wait()

    for p in range(0, planes, step):
        edges = []
        for i in range(step):
            q, k = divmod(p + i, per)
            left, right = got_l[q], got_r[q]
            at = 8 * k
            left = left if at == 0 else pltpu.roll(left, LANES - at, 1)
            right = right if at == 8 else pltpu.roll(right, (LANES - at + 8) % LANES, 1)
            edges.append(jnp.where(lane < 8, left, right))
        hi, lo = split(jnp.concatenate(edges, axis=0))
        got = jnp.dot(jnp.concatenate([hi, lo], axis=1), xe[...], preferred_element_type=jnp.float32)
        value = zb[p:p + step] + (got[:, :LANES] + got[:, LANES:]).reshape(step, rows, LANES)
        if kind == 0:
            out[p:p + step] = moved[p:p + step] / value
        elif kind == 2:
            block, within = divmod(p, nz)
            held = other if within < nb else moved
            at = block * nb + within % nb
            out[p:p + step] = held[at:at + step] / value
        else:
            out[p:p + step] = other[p:p + step] * value

    @pl.when(has_r)
    def _():
        x_copy(0).wait_send()

    @pl.when(has_l)
    def _():
        x_copy(1).wait_send()

    if kind == 1:
        bulk_wait()


def slab_blur(kind, chain, f, other, weights, view, measured):
    planes, rows, _ = f.shape
    vmem = pl.BlockSpec(memory_space=pltpu.VMEM)
    packs = pltpu.VMEM((planes * 8 // LANES, rows, LANES), jnp.float32)
    like = jax.ShapeDtypeStruct
    args = [f] + ([other] if kind else []) + list(weights)
    in_specs = [vmem] * len(args)
    out_shape = [like(f.shape, jnp.float32)]
    scratch = [
        pltpu.VMEM((RZ, rows, LANES), jnp.float32),
        pltpu.VMEM((RZ, rows, LANES), jnp.float32),
        pltpu.VMEM((planes, rows, LANES), jnp.float32),
        packs, packs, packs, packs,
        pltpu.SemaphoreType.DMA((2, CHUNKS)),
        pltpu.SemaphoreType.DMA((2, CHUNKS)),
        pltpu.SemaphoreType.DMA((2,)),
        pltpu.SemaphoreType.DMA((2,)),
    ]
    if kind < 3:
        views, nz, ny, nx = measured.shape
        nb = nz if kind == 0 else nz // 2
        args += [view, measured]
        in_specs += [pl.BlockSpec(memory_space=pltpu.SMEM), pl.BlockSpec(memory_space=pl.ANY)]
        scratch += [
            pltpu.VMEM((views, nb, ny, nx), jnp.float32),
            pltpu.VMEM((nb, ny, nx), jnp.float32),
            pltpu.SemaphoreType.DMA((4,)),
            pltpu.SemaphoreType.DMA((4,)),
            pltpu.SemaphoreType.DMA,
        ]
        if kind == 1:
            out_shape.append(like((2 * nb, rows, LANES), jnp.float32))
        else:
            scratch.append(pltpu.VMEM((2 * nb, rows, LANES), jnp.float32))
    out = pl.pallas_call(
        functools.partial(blur_kernel, kind, chain),
        out_shape=out_shape,
        in_specs=in_specs,
        out_specs=[vmem] * len(out_shape),
        scratch_shapes=scratch,
        compiler_params=pltpu.CompilerParams(collective_id=3 + kind, has_side_effects=True),
    )(*args)
    return out


def slabs(chain, estimate, measured, psf_z, psf_y, psf_x, extents, order):
    views, nz, ny, nx = measured.shape
    current, weights = spread_first(estimate, psf_z, psf_y, psf_x, extents, order)
    seen = [order[p:p + 1] for p in range(views)]
    half = None
    for p in range(views):
        kind = 2 if p else 0
        ratio, = slab_blur(kind, chain, current, half, weights[2 * p], seen[p], measured)
        if p < views - 1:
            current, half = slab_blur(1, chain, ratio, current, weights[2 * p + 1], seen[p + 1], measured)
        else:
            current, = slab_blur(3, chain, ratio, current, weights[2 * p + 1], None, None)
    return gather_back(current, nz, ny, nx)


def on_device(estimate, measured, psf_z, psf_y, psf_x, extents, order):
    n_z, n_y = lax.axis_size("gz"), lax.axis_size("gy")
    nz, ny, nx = estimate.shape
    fits = n_y == 2 and n_z % 4 == 0 and nx == 4 * LANES and nz == 16 and 2 * ny == 64
    if fits:
        return slabs(n_z // 2, estimate, measured, psf_z, psf_y, psf_x, extents, order)
    return general(estimate, measured, psf_z, psf_y, psf_x, extents, order)


def solution(mesh):
    return jax.shard_map(
        on_device,
        mesh=mesh,
        in_specs=(P("gz", "gy", None), P(None, "gz", "gy", None), P(), P(), P(), P(), P()),
        out_specs=P("gz", "gy", None),
        check_vma=False,
    )
```

profile of v0, /device:TPU:19, one launch (start us, length us, event | category | flops | bytes accessed | tf_op | source)
XLA Modules:
  0.0 181.0 jit_solution(11747434298048137640)
XLA Ops:
  0.0 1.5 fusion
  1.5 17.7 %shard_map.73 = (f32[32,64,128]{2,1,0:T(8,128)}, f32[31,8,128]{2,1,0:T(8,128)}, f32[31,8,128]{2,1,0:T(8,128)}, f32[31,8,128]{2,1,0:T(8,128)}, f32[31,8,128]{2,1,...) custom-call(f32[16,32,512]{2,1,0:T(8,128)} %est.1, ...), custom_call_target="tpu_custom_call" | custom-call | tf_op jit(solution)/shard_map/pallas_call | solution.py:225
  19.2 20.9 %shard_map.74.refs_0_ = f32[32,64,128]{2,1,0:T(8,128)} custom-call(f32[32,64,128]{2,1,0:T(8,128)} %get-tuple-element.44.refs_0_.refs_1_, f32[31,8,128]{2,1,0:T(8,128)} %get-tuple-element.45.refs_1_, bf16[64,256]{1,0:T(8,128)(2,1)} %get-tuple-element.46.refs_2_, bf16[256,256]{1,0:T(8,128)(2,1)} %get-tuple-element.47.refs_3_, ...), custom_call_target="tpu_custom_call" | custom-call | tf_op jit(solution)/shard_map/pallas_call | solution.py:550
  40.1 18.0 %shard_map.75 = (f32[32,64,128]{2,1,0:T(8,128)}, f32[16,64,128]{2,1,0:T(8,128)}) custom-call(f32[32,64,128]{2,1,0:T(8,128)} %shard_map.74.refs_0_, f32[32,64,128]{2,1,0:T(8,128)} %get-tuple-element.44.refs_0_.refs_1_, f32[31,8,128]{2,1,0:T(8,128)} %get-tuple-element.49.refs_2_, bf16[64,256]{1,0:T(8,128)(2,1)} %get-tuple-element.50.refs_3_, ...), custom_call_target="tpu_custom_call" | custom-call | tf_op jit(solution)/shard_map/pallas_call | solution.py:550
  58.1 18.1 %shard_map.76.refs_0_ = f32[32,64,128]{2,1,0:T(8,128)} custom-call(f32[32,64,128]{2,1,0:T(8,128)} %get-tuple-element.53.refs_0_.refs_1_, f32[16,64,128]{2,1,0:T(8,128)} %get-tuple-element.54.refs_1_, f32[31,8,128]{2,1,0:T(8,128)} %get-tuple-element.55.refs_2_, bf16[64,256]{1,0:T(8,128)(2,1)} %get-tuple-element.56.refs_3_, ...), custom_call_target="tpu_custom_call" | custom-call | tf_op jit(solution)/shard_map/pallas_call | solution.py:550
  76.2 17.1 %shard_map.77 = (f32[32,64,128]{2,1,0:T(8,128)}, f32[16,64,128]{2,1,0:T(8,128)}) custom-call(f32[32,64,128]{2,1,0:T(8,128)} %shard_map.76.refs_0_, f32[32,64,128]{2,1,0:T(8,128)} %get-tuple-element.53.refs_0_.refs_1_, f32[31,8,128]{2,1,0:T(8,128)} %get-tuple-element.59.refs_2_, bf16[64,256]{1,0:T(8,128)(2,1)} %get-tuple-element.60.refs_3_, ...), custom_call_target="tpu_custom_call" | custom-call | tf_op jit(solution)/shard_map/pallas_call | solution.py:550
  93.3 18.0 %shard_map.78.refs_0_ = f32[32,64,128]{2,1,0:T(8,128)} custom-call(f32[32,64,128]{2,1,0:T(8,128)} %get-tuple-element.63.refs_0_.refs_1_, f32[16,64,128]{2,1,0:T(8,128)} %get-tuple-element.64.refs_1_, f32[31,8,128]{2,1,0:T(8,128)} %get-tuple-element.65.refs_2_, bf16[64,256]{1,0:T(8,128)(2,1)} %get-tuple-element.66.refs_3_, ...), custom_call_target="tpu_custom_call" | custom-call | tf_op jit(solution)/shard_map/pallas_call | solution.py:550
  111.3 17.1 %shard_map.79 = (f32[32,64,128]{2,1,0:T(8,128)}, f32[16,64,128]{2,1,0:T(8,128)}) custom-call(f32[32,64,128]{2,1,0:T(8,128)} %shard_map.78.refs_0_, f32[32,64,128]{2,1,0:T(8,128)} %get-tuple-element.63.refs_0_.refs_1_, f32[31,8,128]{2,1,0:T(8,128)} %get-tuple-element.69.refs_2_, bf16[64,256]{1,0:T(8,128)(2,1)} %get-tuple-element.70.refs_3_, ...), custom_call_target="tpu_custom_call" | custom-call | tf_op jit(solution)/shard_map/pallas_call | solution.py:550
  128.4 18.5 %shard_map.80.refs_0_ = f32[32,64,128]{2,1,0:T(8,128)} custom-call(f32[32,64,128]{2,1,0:T(8,128)} %get-tuple-element.73.refs_0_.refs_1_, f32[16,64,128]{2,1,0:T(8,128)} %get-tuple-element.74.refs_1_, f32[31,8,128]{2,1,0:T(8,128)} %get-tuple-element.75.refs_2_, bf16[64,256]{1,0:T(8,128)(2,1)} %get-tuple-element.76.refs_3_, ...), custom_call_target="tpu_custom_call" | custom-call | tf_op jit(solution)/shard_map/pallas_call | solution.py:550
  147.0 15.7 %shard_map.81.src = f32[32,64,128]{2,1,0:T(8,128)} custom-call(f32[32,64,128]{2,1,0:T(8,128)} %shard_map.80.refs_0_, f32[32,64,128]{2,1,0:T(8,128)} %get-tuple-element.73.refs_0_.refs_1_, f32[31,8,128]{2,1,0:T(8,128)} %get-tuple-element.79.refs_2_, bf16[64,256]{1,0:T(8,128)(2,1)} %get-tuple-element.80.refs_3_, bf16[256,256]{1,0:T(8,128)(2,1)} %get-tuple-element.81.refs_4_, ...), custom_call_target="tpu_custom_call" | custom-call | tf_op jit(solution)/shard_map/pallas_call | solution.py:550
  162.7 16.0 %shard_map.82 = f32[16,32,512]{2,1,0:T(8,128)} custom-call(f32[32,64,128]{2,1,0:T(8,128)} %shard_map.81.src), custom_call_target="tpu_custom_call" | custom-call | tf_op jit(solution)/shard_map/pallas_call | solution.py:151
  178.7 2.3 %copy.9 = f32[16,32,512]{2,1,0:T(8,128)} copy(f32[16,32,512]{2,1,0:T(8,128)} %shard_map.82) | data formatting | bytes 2097152
where the time goes:
time: 182 us; the launch traced here: 181 us
  Pallas kernels  177 us (97%)
  local copies, waits for them, and re-layouts  3.76 us (2%)
    pallas_call x8, Pallas kernels, slab_blur(): pl.pallas_call(functools.partial(blur_kernel, kind, chain), out_shape=out...  144 us
    pallas_call x1, Pallas kernels, spread_first(): pl.pallas_call(functools.partial(first_kernel, nz, ny, views), out_shape=...  17.7 us
    pallas_call x1, Pallas kernels, gather_back(): pl.pallas_call(functools.partial(back_kernel, nz, ny), out_shape=jax.Shap...  16 us

commit v1 on v0

v1 whole, which is shorter than its diff:
```python
import functools
import jax
import jax.numpy as jnp
from jax import lax
from jax.experimental import pallas as pl
from jax.experimental.pallas import tpu as pltpu
from jax.sharding import PartitionSpec as P

MESH = pl.DeviceIdType.MESH
RZ = 15
RL = 7
LANES = 128


def with_halo(value, sides, width):
    for axis, dim in sides:
        size, length = (lax.axis_size(axis), value.shape[dim])
        up = [(i, (i + 1) % size) for i in range(size - 1)]
        down = [(j, i) for i, j in up]
        last = lax.slice_in_dim(value, length - width, length, axis=dim)
        initial = lax.slice_in_dim(value, 0, width, axis=dim)
        before = lax.ppermute(last, axis, up)
        after = lax.ppermute(initial, axis, down)
        value = jnp.concatenate([before, value, after], axis=dim)
    return value


def line_taps(profile, reach_cells, tap_reach):
    offsets = jnp.arange(2 * tap_reach + 1, dtype=jnp.int32) - tap_reach
    kept = jnp.where(jnp.abs(offsets) <= reach_cells, profile, jnp.zeros_like(profile))
    return kept / jnp.sum(kept)


def correlate_padded(padded, weights, along_axis, tap_reach, length, flipped):
    total = None
    for offset in range(2 * tap_reach + 1):
        start = 2 * tap_reach - offset if flipped else offset
        piece = lax.slice_in_dim(padded, start, start + length, axis=along_axis)
        term = weights[offset] * piece
        total = term if total is None else total + term
    return total


def blur(field, weights_z, weights_y, weights_x, flipped):
    padded = with_halo(field, (("gz", 0),), RZ)
    result = correlate_padded(padded, weights_z, 0, RZ, field.shape[0], flipped)
    widened = with_halo(result, (("gy", 1),), RL)
    result = correlate_padded(widened, weights_y, 1, RL, field.shape[1], flipped)
    result = jnp.pad(result, ((0, 0), (0, 0), (RL, RL)))
    return correlate_padded(result, weights_x, 2, RL, field.shape[2], flipped)


def general(estimate, measured, psf_z, psf_y, psf_x, extents, order):
    current = estimate
    for position in range(measured.shape[0]):
        view = order[position]
        radii = (extents[view] - 1) // 2
        weights_z = line_taps(psf_z[view], radii[0], RZ)
        weights_y = line_taps(psf_y[view], radii[1], RL)
        weights_x = line_taps(psf_x[view], radii[2], RL)
        recorded = lax.dynamic_index_in_dim(measured, view, 0, keepdims=False)
        blurred = blur(current, weights_z, weights_y, weights_x, False)
        ratio = recorded / blurred
        current = current * blur(ratio, weights_z, weights_y, weights_x, True)
    return current


def place():
    g = lax.axis_index("gz")
    w = lax.axis_index("gy")
    return g // 4, (g // 2) % 2, g % 2, w


def slab_of(a, w):
    return 2 * a + lax.rem(w + a, 2)


def group_peers():
    h, a, c, w = place()
    peers = []
    for k in range(1, 8):
        da, dc, dw = k // 4, (k // 2) % 2, k % 2
        device = (4 * h + 2 * lax.rem(a + da, 2) + lax.rem(c + dc, 2), lax.rem(w + dw, 2))
        peers.append(device)
    return peers


def taps_of(profile, view, radius, reach):
    kept = []
    for k in range(2 * reach + 1):
        value = jnp.full((8, LANES), profile[view, k], jnp.float32)
        kept.append(jnp.where(abs(k - reach) <= radius, value, jnp.zeros_like(value)))
    total = kept[0]
    for value in kept[1:]:
        total = total + value
    return [value / total for value in kept]


def band(taps, which):
    total = jnp.zeros(which.shape, jnp.float32)
    for k, tap in enumerate(taps):
        total = jnp.where(which == k, tap[0:1, :], total)
    return split(total)


def split(value):
    hi = value.astype(jnp.bfloat16)
    lo = (value - hi.astype(jnp.float32)).astype(jnp.bfloat16)
    return hi, lo


ROWS = 8
LAG = 3


def wavefront_kernel(chain, nz, ny, views, est, measured, psf_z, psf_y, psf_x, extents, order, out,
                     wz, wy, xm, xe, f, zh, zb, yb, pack, got, stage, chosen, moved,
                     zs, zr, xs, xr, es, er, bs, br, gs, gr, el, gl, fl):
    h, a, c, w = place()
    zi = 2 * h + c
    s = slab_of(a, w)
    planes = 2 * nz
    chunks = 2 * ny // ROWS
    own = ny // ROWS
    blurs = 2 * views
    last = blurs * chunks
    has_dn, has_up = zi > 0, zi < chain - 1
    has_l, has_r = s > 0, s < 3
    home = c == a
    away = c != a

    def z_dev(i):
        return (4 * (i // 2) + 2 * a + lax.rem(i, 2), w)

    def x_dev(i):
        b = i // 2
        return (4 * h + 2 * b + c, lax.rem(i + b, 2))

    up, dn = z_dev(lax.rem(zi + 1, chain)), z_dev(lax.rem(zi + chain - 1, chain))
    lf, rt = x_dev(lax.rem(s + 3, 4)), x_dev(lax.rem(s + 1, 4))
    far_there = jnp.where(c == 1, h < chain // 2 - 1, h > 0)
    far = z_dev(jnp.where(c == 1, lax.rem(zi + 1, chain), lax.rem(zi + chain - 1, chain)))

    barrier = pltpu.get_barrier_semaphore()
    for device in group_peers():
        pl.semaphore_signal(barrier, inc=1, device_id=device, device_id_type=MESH)

    @pl.when(far_there)
    def _():
        pl.semaphore_signal(barrier, inc=1, device_id=far, device_id_type=MESH)

    fetch = pltpu.make_async_copy(measured, stage, fl)
    fetch.start()
    pl.semaphore_wait(barrier, 7 + far_there.astype(jnp.int32))

    def remote(src, dst, send, recv, device):
        return pltpu.make_async_remote_copy(src_ref=src, dst_ref=dst, send_sem=send, recv_sem=recv,
                                            device_id=device, device_id_type=MESH)

    def rows8(r):
        return pl.ds(pl.multiple_of(ROWS * r, ROWS), ROWS)

    def outward(r, k):
        da, dw = k // 2, k % 2
        ta, tw = lax.rem(c + da, 2), lax.rem(w + dw, 2)
        x0 = pl.multiple_of(LANES * slab_of(ta, tw), LANES)
        return (slice(None), rows8(r), pl.ds(x0, LANES)), (own * w + r, pl.ds(nz * c, nz)), (4 * h + 2 * ta + a, tw)

    def est_copy(r, k):
        there, here, device = outward(r, k)
        return remote(est.at[there], f.at[(0,) + here], es.at[r, k], er.at[r, k], device)

    def est_local(r):
        there, here, _ = outward(r, 0)
        return pltpu.make_async_copy(est.at[there], f.at[(0,) + here], el.at[r])

    def bulk(p, r, k):
        there, here, device = outward(r, k)
        return remote(chosen.at[(p,) + there], moved.at[(p,) + here], bs.at[p, r, k], br.at[p, r, k], device)

    def back(j, tc):
        tw, r = j // own, lax.rem(j, own)
        k = 2 * lax.rem(tc + a, 2) + lax.rem(tw + w, 2)
        x0 = pl.multiple_of(LANES * s, LANES)
        src = f.at[0, j, pl.ds(nz * tc, nz)]
        dst = out.at[:, rows8(r), pl.ds(x0, LANES)]
        return (remote(src, dst, gs.at[r, k], gr.at[r, k], (4 * h + 2 * c + tc, tw)),
                pltpu.make_async_copy(src, dst, gl.at[r]), jnp.logical_and(home, k == 0))

    def z_copy(side, par, j):
        if side == 0:
            return remote(f.at[par, j, pl.ds(planes - RZ, RZ)], zh.at[0, par, j], zs.at[0, par, j], zr.at[0, par, j], up)
        return remote(f.at[par, j, pl.ds(0, RZ)], zh.at[1, par, j], zs.at[1, par, j], zr.at[1, par, j], dn)

    def x_copy(side, par, j):
        if side == 0:
            return remote(pack.at[1, par, j], got.at[0, par, j], xs.at[0, par, j], xr.at[0, par, j], rt)
        return remote(pack.at[0, par, j], got.at[1, par, j], xs.at[1, par, j], xr.at[1, par, j], lf)

    def guarded(cond, act):
        @pl.when(cond)
        def _():
            act()

    for r in range(own):
        for k in range(1, 4):
            est_copy(r, k).start()
        guarded(away, lambda: est_copy(r, 0).start())
        guarded(home, lambda: est_local(r).start())

    build_weights(views, psf_z, psf_y, psf_x, extents, order, wz, wy, xm, xe)

    zb[...] = jnp.zeros_like(zb)

    def clear(ref, side):
        def one(i, carry):
            ref[side, i // chunks, lax.rem(i, chunks)] = jnp.zeros(ref.shape[3:], jnp.float32)
            return carry

        lax.fori_loop(0, 2 * chunks, one, 0)

    guarded(jnp.logical_not(has_dn), lambda: clear(zh, 0))
    guarded(jnp.logical_not(has_up), lambda: clear(zh, 1))
    guarded(jnp.logical_not(has_l), lambda: clear(got, 0))
    guarded(jnp.logical_not(has_r), lambda: clear(got, 1))

    fetch.wait()
    for p in range(views):
        def pick(i, carry):
            chosen[p, i] = stage[order[p], i]
            return carry

        lax.fori_loop(0, nz, pick, 0)

    def keep():
        x0 = pl.multiple_of(LANES * slab_of(c, w), LANES)
        for p in range(views):
            for r in range(own):
                moved[p, own * w + r, pl.ds(nz * c, nz)] = chosen[p, :, r * ROWS:(r + 1) * ROWS, pl.ds(x0, LANES)]

    guarded(home, keep)

    def send_z(par, j):
        guarded(has_up, lambda: z_copy(0, par, j).start())
        guarded(has_dn, lambda: z_copy(1, par, j).start())

    def enter(i):
        guarded(home, lambda: est_local(i).wait())
        guarded(away, lambda: est_copy(i, 0).wait_recv())
        for k in range(1, 4):
            est_copy(i, k).wait_recv()
        send_z(0, i)
        send_z(0, i + own)

    lane = lax.broadcasted_iota(jnp.int32, (ROWS, LANES), 1)
    per = LANES // 8
    half = 16

    def z_stage(t):
        k = t // chunks
        j = t - k * chunks
        par = lax.rem(k, 2)
        guarded(has_dn, lambda: z_copy(0, par, j).wait_recv())
        guarded(has_up, lambda: z_copy(1, par, j).wait_recv())
        taps = [wz[k, i] for i in range(2 * RZ + 1)]
        ys = pl.ds(pl.multiple_of(ROWS * j + ROWS, ROWS), ROWS)
        for first in range(0, planes, half):
            acc = [None] * half
            for p in range(first, first + half + 2 * RZ):
                if p < RZ:
                    v = zh[0, par, j, p]
                elif p < RZ + planes:
                    v = f[par, j, p - RZ]
                else:
                    v = zh[1, par, j, p - RZ - planes]
                for o in range(half):
                    i = p - first - o
                    if 0 <= i <= 2 * RZ:
                        term = taps[i] * v
                        acc[o] = term if acc[o] is None else acc[o] + term
            for o in range(half):
                zb[first + o, ys, :] = acc[o]

    def y_stage(t):
        k = t // chunks
        j = t - k * chunks
        par = lax.rem(k, 2)

        def reuse():
            guarded(has_r, lambda: x_copy(0, par, j).wait_send())
            guarded(has_l, lambda: x_copy(1, par, j).wait_send())

        guarded(k >= 2, reuse)
        taps = [wy[k, i] for i in range(2 * RL + 1)]
        base = pl.multiple_of(ROWS * j, ROWS)
        for q in range(planes // per):
            packed_l = packed_r = None
            for i in range(per):
                p = q * per + i
                value = None
                for o in range(2 * RL + 1):
                    term = taps[o] * zb[p, pl.ds(base + (o + ROWS - RL), ROWS), :]
                    value = term if value is None else value + term
                yb[j, p] = value
                at = 8 * i
                left = value if at == 0 else pltpu.roll(value, at, 1)
                right = pltpu.roll(value, (at + 8) % LANES, 1) if at + 8 < LANES else value
                packed_l = left if packed_l is None else jnp.where(lane >= at, left, packed_l)
                packed_r = right if packed_r is None else jnp.where(lane >= at, right, packed_r)
            pack[0, par, j, q] = packed_l
            pack[1, par, j, q] = packed_r
        guarded(has_r, lambda: x_copy(0, par, j).start())
        guarded(has_l, lambda: x_copy(1, par, j).start())

    step = 8

    def x_stage(t):
        k = t // chunks
        j = t - k * chunks
        par = lax.rem(k, 2)
        even = par == 0
        p_view = k // 2
        nxt = lax.rem(k + 1, 2)
        guarded(has_l, lambda: x_copy(0, par, j).wait_recv())
        guarded(has_r, lambda: x_copy(1, par, j).wait_recv())

        def sent():
            guarded(has_up, lambda: z_copy(0, nxt, j).wait_send())
            guarded(has_dn, lambda: z_copy(1, nxt, j).wait_send())

        guarded(k >= 1, sent)

        def body(divide):
            if divide:
                dw = lax.rem(w + j // own, 2)
                r = lax.rem(j, own)
                for da in range(2):
                    if da == 0:
                        guarded(jnp.logical_or(away, dw > 0), lambda: bulk(p_view, r, dw).wait_recv())
                    else:
                        bulk(p_view, r, 2 + dw).wait_recv()
            for p in range(0, planes, step):
                edges = []
                for i in range(step):
                    q, n = divmod(p + i, per)
                    left, right = got[0, par, j, q], got[1, par, j, q]
                    at = 8 * n
                    left = left if at == 0 else pltpu.roll(left, LANES - at, 1)
                    right = right if at == 8 else pltpu.roll(right, (LANES - at + 8) % LANES, 1)
                    edges.append(jnp.where(lane < 8, left, right))
                ehi, elo = split(jnp.concatenate(edges, axis=0))
                hi, lo = split(yb[j, p:p + step].reshape(step * ROWS, LANES))
                value = jnp.dot(jnp.concatenate([hi, lo], axis=1), xm[k], preferred_element_type=jnp.float32)
                value = value + jnp.dot(jnp.concatenate([ehi, elo], axis=1), xe[k], preferred_element_type=jnp.float32)
                value = (value[:, :LANES] + value[:, LANES:]).reshape(step, ROWS, LANES)
                if divide:
                    f[1, j, p:p + step] = moved[p_view, j, p:p + step] / value
                else:
                    f[0, j, p:p + step] = f[0, j, p:p + step] * value

        guarded(even, lambda: body(True))
        guarded(jnp.logical_not(even), lambda: body(False))

        def finish():
            for tc in range(2):
                far_copy, near_copy, local = back(j, tc)
                guarded(local, lambda: near_copy.start())
                guarded(jnp.logical_not(local), lambda: far_copy.start())

        guarded(k < blurs - 1, lambda: send_z(nxt, j))
        guarded(k == blurs - 1, finish)

    def feed(t):
        n = t - (LAG + 2)
        p = 1 + n // (4 * own)
        q = lax.rem(n, 4 * own)
        k = lax.rem(q, 4)
        guarded(jnp.logical_or(away, k > 0), lambda: bulk(p, q // 4, k).start())

    def feed_first(r):
        guarded(away, lambda: bulk(0, r, 0).start())
        for k in range(1, 4):
            bulk(0, r, k).start()

    enter(0)
    enter(1)
    for t in range(LAG + 1):
        if t < own:
            feed_first(t)
        z_stage(t)
        if t:
            y_stage(t - 1)
        if 2 + t < own:
            enter(2 + t)

    def main(t, carry):
        n = t - (LAG + 2)
        guarded(jnp.logical_and(n >= 0, n < 4 * own * (views - 1)), lambda: feed(t))
        z_stage(t)
        y_stage(t - 1)
        x_stage(t - 1 - LAG)
        return carry

    lax.fori_loop(LAG + 1, last, main, 0)
    y_stage(jnp.int32(last - 1))

    def drain(t, carry):
        x_stage(t)
        return carry

    lax.fori_loop(last - 1 - LAG, last, drain, 0)

    def settle(j, carry):
        par = (blurs - 1) % 2
        guarded(has_up, lambda: z_copy(0, par, j).wait_send())
        guarded(has_dn, lambda: z_copy(1, par, j).wait_send())
        for side in range(2):
            guarded(has_r, lambda: x_copy(0, side, j).wait_send())
            guarded(has_l, lambda: x_copy(1, side, j).wait_send())
        for tc in range(2):
            far_copy, near_copy, local = back(j, tc)
            guarded(local, lambda: near_copy.wait())
            guarded(jnp.logical_not(local), lambda: far_copy.wait())
        return carry

    lax.fori_loop(0, chunks, settle, 0)

    def delivered(i, carry):
        p, q = i // (4 * own), lax.rem(i, 4 * own)
        k = lax.rem(q, 4)
        guarded(jnp.logical_or(away, k > 0), lambda: bulk(p, q // 4, k).wait_send())
        return carry

    lax.fori_loop(0, 4 * own * views, delivered, 0)
    for r in range(own):
        guarded(away, lambda: est_copy(r, 0).wait_send())
        for k in range(1, 4):
            est_copy(r, k).wait_send()


def build_weights(views, psf_z, psf_y, psf_x, extents, order, wz, wy, xm, xe):
    def iota(shape, dim):
        return lax.broadcasted_iota(jnp.int32, shape, dim)

    x_which = iota((LANES, LANES), 0) - iota((LANES, LANES), 1) + RL
    r = iota((16, LANES), 0)
    e_which = jnp.where(r < 8, r - 8, r + (LANES - 8)) - iota((16, LANES), 1) + RL
    for p in range(views):
        view = order[p]
        tz = taps_of(psf_z, view, (extents[view, 0] - 1) // 2, RZ)
        ty = taps_of(psf_y, view, (extents[view, 1] - 1) // 2, RL)
        tx = taps_of(psf_x, view, (extents[view, 2] - 1) // 2, RL)
        for i in (2 * p, 2 * p + 1):
            for k in range(2 * RZ + 1):
                wz[i, k] = tz[k]
            for k in range(2 * RL + 1):
                wy[i, k] = ty[k]
            hi, lo = band(tx, x_which)
            for top in (0, LANES):
                xm[i, top:top + LANES, :LANES] = hi
                xm[i, top:top + LANES, LANES:] = lo
            hi, lo = band(tx, e_which)
            xe[i] = jnp.zeros(xe.shape[1:], xe.dtype)
            for top in (0, LANES):
                xe[i, top:top + 16, :LANES] = hi
                xe[i, top:top + 16, LANES:] = lo
            tz, ty, tx = tz[::-1], ty[::-1], tx[::-1]


def slabs(chain, estimate, measured, psf_z, psf_y, psf_x, extents, order):
    views, nz, ny, nx = measured.shape
    planes, rows = 2 * nz, 2 * ny
    chunks, own, blurs = rows // ROWS, ny // ROWS, 2 * views
    f32, bf16 = jnp.float32, jnp.bfloat16
    smem = pl.BlockSpec(memory_space=pltpu.SMEM)
    anywhere = pl.BlockSpec(memory_space=pl.ANY)
    dma = pltpu.SemaphoreType.DMA
    packs = pltpu.VMEM((2, 2, chunks, planes * 8 // LANES, ROWS, LANES), f32)
    return pl.pallas_call(
        functools.partial(wavefront_kernel, chain, nz, ny, views),
        out_shape=jax.ShapeDtypeStruct((nz, ny, nx), f32),
        in_specs=[anywhere] * 2 + [smem] * 5,
        out_specs=anywhere,
        scratch_shapes=[
            pltpu.VMEM((blurs, 2 * RZ + 1, ROWS, LANES), f32),
            pltpu.VMEM((blurs, 2 * RL + 1, ROWS, LANES), f32),
            pltpu.VMEM((blurs, 2 * LANES, 2 * LANES), bf16),
            pltpu.VMEM((blurs, 2 * LANES, 2 * LANES), bf16),
            pltpu.VMEM((2, chunks, planes, ROWS, LANES), f32),
            pltpu.VMEM((2, 2, chunks, RZ, ROWS, LANES), f32),
            pltpu.VMEM((planes, rows + 2 * ROWS, LANES), f32),
            pltpu.VMEM((chunks, planes, ROWS, LANES), f32),
            packs, packs,
            pltpu.VMEM((views, nz, ny, nx), f32),
            pltpu.VMEM((views, nz, ny, nx), f32),
            pltpu.VMEM((views, chunks, planes, ROWS, LANES), f32),
            dma((2, 2, chunks)), dma((2, 2, chunks)),
            dma((2, 2, chunks)), dma((2, 2, chunks)),
            dma((own, 4)), dma((own, 4)),
            dma((views, own, 4)), dma((views, own, 4)),
            dma((own, 4)), dma((own, 4)),
            dma((own,)), dma((own,)), dma,
        ],
        compiler_params=pltpu.CompilerParams(collective_id=1, has_side_effects=True),
    )(estimate, measured, psf_z, psf_y, psf_x, extents, order)


def on_device(estimate, measured, psf_z, psf_y, psf_x, extents, order):
    n_z, n_y = lax.axis_size("gz"), lax.axis_size("gy")
    nz, ny, nx = estimate.shape
    fits = n_y == 2 and n_z % 4 == 0 and nx == 4 * LANES and nz == 16 and 2 * ny == 64
    if fits:
        return slabs(n_z // 2, estimate, measured, psf_z, psf_y, psf_x, extents, order)
    return general(estimate, measured, psf_z, psf_y, psf_x, extents, order)


def solution(mesh):
    return jax.shard_map(
        on_device,
        mesh=mesh,
        in_specs=(P("gz", "gy", None), P(None, "gz", "gy", None), P(), P(), P(), P(), P()),
        out_specs=P("gz", "gy", None),
        check_vma=False,
    )
```

time: 182 us -> 120 us (0.66)
  Pallas kernels: 177 us -> 117 us
    pallas_call x10 -> x1, Pallas kernels: 177 us -> 117 us  [slabs(): pl.pallas_call(functools.partial(wavefront_kernel, chain, nz, ny, views),...]
where the time goes in v1:
time: 120 us; the launch traced here: 119 us
  Pallas kernels  117 us (98%)
  local copies, waits for them, and re-layouts  2.29 us (2%)
    pallas_call x1, Pallas kernels, slabs(): pl.pallas_call(functools.partial(wavefront_kernel, chain, nz, ny, views),...  117 us

profile of v1, /device:TPU:19, one launch (start us, length us, event | category | flops | bytes accessed | tf_op | source)
XLA Modules:
  0.0 119.4 jit_solution(7534840308995705599)
XLA Ops:
  0.0 117.1 %shard_map.73 = f32[16,32,512]{2,1,0:T(8,128)} custom-call(f32[16,32,512]{2,1,0:T(8,128)} %est.1, f32[4,16,32,512]{3,2,1,0:T(8,128)} %measured.1, f32[4,31]{1,0:T(4,128)} %psf_z.1, f32[4,15]{1,0:T(4,128)} %psf_y.1, f32[4,15]{1,0:T(4,128)} %psf_x.1, s32[4,3]{1,0:T(4,128)} %extents.1, s32[4]{0:T(128)} %order.1), custom_call_target="tpu_custom_call" | custom-call | tf_op jit(solution)/shard_map/pallas_call | solution.py:479
  117.1 2.3 %copy.9 = f32[16,32,512]{2,1,0:T(8,128)} copy(f32[16,32,512]{2,1,0:T(8,128)} %shard_map.73) | data formatting | bytes 2097152

commit v2 on v1

v2 whole, which is shorter than its diff:
```python
import functools
import jax
import jax.numpy as jnp
from jax import lax
from jax.experimental import pallas as pl
from jax.experimental.pallas import tpu as pltpu
from jax.sharding import PartitionSpec as P

MESH = pl.DeviceIdType.MESH
RZ = 15
RL = 7
LANES = 128


def with_halo(value, sides, width):
    for axis, dim in sides:
        size, length = (lax.axis_size(axis), value.shape[dim])
        up = [(i, (i + 1) % size) for i in range(size - 1)]
        down = [(j, i) for i, j in up]
        last = lax.slice_in_dim(value, length - width, length, axis=dim)
        initial = lax.slice_in_dim(value, 0, width, axis=dim)
        before = lax.ppermute(last, axis, up)
        after = lax.ppermute(initial, axis, down)
        value = jnp.concatenate([before, value, after], axis=dim)
    return value


def line_taps(profile, reach_cells, tap_reach):
    offsets = jnp.arange(2 * tap_reach + 1, dtype=jnp.int32) - tap_reach
    kept = jnp.where(jnp.abs(offsets) <= reach_cells, profile, jnp.zeros_like(profile))
    return kept / jnp.sum(kept)


def correlate_padded(padded, weights, along_axis, tap_reach, length, flipped):
    total = None
    for offset in range(2 * tap_reach + 1):
        start = 2 * tap_reach - offset if flipped else offset
        piece = lax.slice_in_dim(padded, start, start + length, axis=along_axis)
        term = weights[offset] * piece
        total = term if total is None else total + term
    return total


def blur(field, weights_z, weights_y, weights_x, flipped):
    padded = with_halo(field, (("gz", 0),), RZ)
    result = correlate_padded(padded, weights_z, 0, RZ, field.shape[0], flipped)
    widened = with_halo(result, (("gy", 1),), RL)
    result = correlate_padded(widened, weights_y, 1, RL, field.shape[1], flipped)
    result = jnp.pad(result, ((0, 0), (0, 0), (RL, RL)))
    return correlate_padded(result, weights_x, 2, RL, field.shape[2], flipped)


def general(estimate, measured, psf_z, psf_y, psf_x, extents, order):
    current = estimate
    for position in range(measured.shape[0]):
        view = order[position]
        radii = (extents[view] - 1) // 2
        weights_z = line_taps(psf_z[view], radii[0], RZ)
        weights_y = line_taps(psf_y[view], radii[1], RL)
        weights_x = line_taps(psf_x[view], radii[2], RL)
        recorded = lax.dynamic_index_in_dim(measured, view, 0, keepdims=False)
        blurred = blur(current, weights_z, weights_y, weights_x, False)
        ratio = recorded / blurred
        current = current * blur(ratio, weights_z, weights_y, weights_x, True)
    return current


def place():
    g = lax.axis_index("gz")
    w = lax.axis_index("gy")
    return g // 4, (g // 2) % 2, g % 2, w


def slab_of(a, w):
    return 2 * a + lax.rem(w + a, 2)


def group_peers():
    h, a, c, w = place()
    peers = []
    for k in range(1, 8):
        da, dc, dw = k // 4, (k // 2) % 2, k % 2
        device = (4 * h + 2 * lax.rem(a + da, 2) + lax.rem(c + dc, 2), lax.rem(w + dw, 2))
        peers.append(device)
    return peers


def taps_of(profile, view, radius, reach):
    kept = []
    for k in range(2 * reach + 1):
        value = jnp.full((8, LANES), profile[view, k], jnp.float32)
        kept.append(jnp.where(abs(k - reach) <= radius, value, jnp.zeros_like(value)))
    total = kept[0]
    for value in kept[1:]:
        total = total + value
    return [value / total for value in kept]


def band(taps, which):
    total = jnp.zeros(which.shape, jnp.float32)
    for k, tap in enumerate(taps):
        total = jnp.where(which == k, tap[0:1, :], total)
    return split(total)


def split(value):
    hi = value.astype(jnp.bfloat16)
    lo = (value - hi.astype(jnp.float32)).astype(jnp.bfloat16)
    return hi, lo


ROWS = 8
PIECES = 4
GROUPS = 2
WAYS = [(1, -1), (-1, -1), (1, 1), (-1, 1), (0, -1), (0, 1), (1, 0), (-1, 0)]


def wavefront_kernel(chain, nz, ny, views, est, measured, psf_z, psf_y, psf_x, extents, order, out,
                     wz, wy, xm, xe, f, zh, xb, zb, pack, got, stage, chosen, moved,
                     hs, hr, es, er, bs, br, gs, gr, el, gl, fl):
    h, a, c, w = place()
    zi = 2 * h + c
    s = slab_of(a, w)
    planes = 2 * nz
    chunks = 2 * ny // ROWS
    own = ny // ROWS
    home, away = c == a, c != a
    there_z = {1: zi < chain - 1, -1: zi > 0}
    there_x = {1: s < 3, -1: s > 0}

    def there(dz, dx):
        conds = ([there_z[dz]] if dz else []) + ([there_x[dx]] if dx else [])
        return conds[0] if len(conds) == 1 else jnp.logical_and(*conds)

    def device_at(dz, dx):
        z = lax.rem(zi + dz + chain, chain)
        x = lax.rem(s + dx + 4, 4)
        b = x // 2
        return (4 * (z // 2) + 2 * b + lax.rem(z, 2), lax.rem(x + b, 2))

    devices = [device_at(dz, dx) for dz, dx in WAYS]
    sends = [there(dz, dx) for dz, dx in WAYS]
    comes = [there(-dz, -dx) for dz, dx in WAYS]

    def guarded(cond, act):
        @pl.when(cond)
        def _():
            act()

    barrier = pltpu.get_barrier_semaphore()

    def greet(device):
        pl.semaphore_signal(barrier, inc=1, device_id=device, device_id_type=MESH)

    for device in group_peers():
        greet(device)
    count = jnp.int32(7)
    for i, (dz, dx) in enumerate(WAYS):
        if dz:
            other = jnp.logical_and(sends[i], (c == 1) if dz > 0 else (c == 0))
            guarded(other, lambda: greet(devices[i]))
            count = count + other.astype(jnp.int32)
    fetch = pltpu.make_async_copy(measured, stage, fl)
    fetch.start()
    pl.semaphore_wait(barrier, count)

    def remote(src, dst, send, recv, device):
        return pltpu.make_async_remote_copy(src_ref=src, dst_ref=dst, send_sem=send, recv_sem=recv,
                                            device_id=device, device_id_type=MESH)

    def outward(r, k):
        da, dw = k // 2, k % 2
        ta, tw = lax.rem(c + da, 2), lax.rem(w + dw, 2)
        x0 = pl.multiple_of(LANES * slab_of(ta, tw), LANES)
        return ((slice(None), pl.ds(ROWS * r, ROWS), pl.ds(x0, LANES)),
                (own * w + r, pl.ds(nz * c, nz)), (4 * h + 2 * ta + a, tw))

    def est_copy(r, k):
        src, dst, device = outward(r, k)
        return remote(est.at[src], f.at[(0,) + dst], es.at[r, k], er.at[r, k], device)

    def est_local(r):
        src, dst, _ = outward(r, 0)
        return pltpu.make_async_copy(est.at[src], f.at[(0,) + dst], el.at[r])

    def bulk(p, r, k):
        src, dst, device = outward(r, k)
        return remote(chosen.at[(p,) + src], moved.at[(p,) + dst], bs.at[p, r, k], br.at[p, r, k], device)

    def bulk_start(p, r, u, on=None):
        k = 2 * (u // 2) + lax.rem(u % 2 + away.astype(jnp.int32), 2)
        real = jnp.logical_or(away, k > 0)
        guarded(real if on is None else jnp.logical_and(real, on), lambda: bulk(p, r, k).start())

    def back(j, tc):
        tw, r = j // own, j % own
        k = 2 * lax.rem(tc + a, 2) + lax.rem(tw + w, 2)
        x0 = pl.multiple_of(LANES * s, LANES)
        src = f.at[0, j, pl.ds(nz * tc, nz)]
        dst = out.at[:, pl.ds(ROWS * r, ROWS), pl.ds(x0, LANES)]
        return (remote(src, dst, gs.at[r, k], gr.at[r, k], (4 * h + 2 * c + tc, tw)),
                pltpu.make_async_copy(src, dst, gl.at[r]), jnp.logical_and(home, k == 0))

    def halo(i, par, j):
        dz, dx = WAYS[i]
        if dx == 0:
            src = f.at[par, j, pl.ds(planes - RZ if dz > 0 else 0, RZ)]
            dst = zh.at[0 if dz > 0 else 1, par, j]
        else:
            mine, theirs = (0, 1) if dx < 0 else (1, 0)
            if dz == 0:
                src, dst = pack.at[mine, par, j], got.at[theirs, par, j, pl.ds(1, 2)]
            elif dz > 0:
                src, dst = pack.at[mine, par, j, pl.ds(1, 1)], got.at[theirs, par, j, pl.ds(0, 1)]
            else:
                src, dst = pack.at[mine, par, j, pl.ds(0, 1)], got.at[theirs, par, j, pl.ds(3, 1)]
        return remote(src, dst, hs.at[i, par, j], hr.at[i, par, j], devices[i])

    def emit(par, j, on=None):
        for i in range(len(WAYS)):
            cond = sends[i] if on is None else jnp.logical_and(sends[i], on)
            guarded(cond, lambda: halo(i, par, j).start())

    def arrive(par, j):
        for i in range(len(WAYS)):
            guarded(comes[i], lambda: halo(i, par, j).wait_recv())

    def gone(par, j, on=None):
        for i in range(len(WAYS)):
            cond = sends[i] if on is None else jnp.logical_and(sends[i], on)
            guarded(cond, lambda: halo(i, par, j).wait_send())

    for r in range(own):
        for k in range(1, 4):
            est_copy(r, k).start()
        guarded(away, lambda: est_copy(r, 0).start())
        guarded(home, lambda: est_local(r).start())

    build_weights(views, psf_z, psf_y, psf_x, extents, order, wz, wy, xm, xe)

    zb[...] = jnp.zeros_like(zb)

    def clear(ref, side):
        def one(i, carry):
            ref[side, i // chunks, lax.rem(i, chunks)] = jnp.zeros(ref.shape[3:], jnp.float32)
            return carry

        lax.fori_loop(0, 2 * chunks, one, 0)

    def clear_corner(q):
        def one(i, carry):
            for side in range(2):
                got[side, i // chunks, lax.rem(i, chunks), q] = jnp.zeros((ROWS, LANES), jnp.float32)
            return carry

        lax.fori_loop(0, 2 * chunks, one, 0)

    for side, d in ((0, -1), (1, 1)):
        guarded(jnp.logical_not(there_z[d]), lambda: clear(zh, side))
        guarded(jnp.logical_not(there_z[d]), lambda: clear_corner(3 * side))
        guarded(jnp.logical_not(there_x[d]), lambda: clear(got, side))

    fetch.wait()
    for p in range(views):
        def pick(i, carry):
            chosen[p, i] = stage[order[p], i]
            return carry

        lax.fori_loop(0, nz, pick, 0)

    def keep():
        x0 = pl.multiple_of(LANES * slab_of(c, w), LANES)
        for p in range(views):
            for r in range(own):
                moved[p, own * w + r, pl.ds(nz * c, nz)] = chosen[p, :, r * ROWS:(r + 1) * ROWS, pl.ds(x0, LANES)]

    guarded(home, keep)

    lane = lax.broadcasted_iota(jnp.int32, (ROWS, LANES), 1)
    per = LANES // 8
    half = 16

    def pack_edges(values, par, j):
        for q in range(planes // per):
            packed_l = packed_r = None
            for i in range(per):
                value = values[q * per + i]
                at = 8 * i
                left = value if at == 0 else pltpu.roll(value, at, 1)
                right = pltpu.roll(value, (at + 8) % LANES, 1) if at + 8 < LANES else value
                packed_l = left if packed_l is None else jnp.where(lane >= at, left, packed_l)
                packed_r = right if packed_r is None else jnp.where(lane >= at, right, packed_r)
            pack[0, par, j, q] = packed_l
            pack[1, par, j, q] = packed_r

    def enter(i):
        guarded(home, lambda: est_local(i).wait())
        guarded(away, lambda: est_copy(i, 0).wait_recv())
        for k in range(1, 4):
            est_copy(i, k).wait_recv()
        for j in (i, i + own):
            pack_edges([f[0, j, p] for p in range(planes)], 0, j)
            emit(0, j)

    wide = planes + 2 * RZ

    def x_stage(k, par, j):
        rows = jnp.concatenate([zh[0, par, j].reshape(RZ * ROWS, LANES), f[par, j].reshape(planes * ROWS, LANES),
                                zh[1, par, j].reshape(RZ * ROWS, LANES)], axis=0)
        m = wide // GROUPS
        for g in range(GROUPS):
            edges = []
            for i in range(m):
                q, n = divmod(g * m + i + 1, per)
                left, right = got[0, par, j, q], got[1, par, j, q]
                at = 8 * n
                left = left if at == 0 else pltpu.roll(left, LANES - at, 1)
                right = right if at == 8 else pltpu.roll(right, (LANES - at + 8) % LANES, 1)
                edges.append(jnp.where(lane < 8, left, right))
            ehi, elo = split(jnp.concatenate(edges, axis=0))
            hi, lo = split(rows[g * m * ROWS:(g + 1) * m * ROWS])
            value = jnp.dot(jnp.concatenate([hi, lo], axis=1), xm[k], preferred_element_type=jnp.float32)
            value = value + jnp.dot(jnp.concatenate([ehi, elo], axis=1), xe[k], preferred_element_type=jnp.float32)
            xb[j % 2, g * m:(g + 1) * m] = (value[:, :LANES] + value[:, LANES:]).reshape(m, ROWS, LANES)

    def z_stage(k, j):
        taps = [wz[k, i] for i in range(2 * RZ + 1)]
        for first in range(0, planes, half):
            acc = [None] * half
            for p in range(first, first + half + 2 * RZ):
                v = xb[j % 2, p]
                for o in range(half):
                    i = p - first - o
                    if 0 <= i <= 2 * RZ:
                        term = taps[i] * v
                        acc[o] = term if acc[o] is None else acc[o] + term
            for o in range(half):
                zb[first + o, ROWS * (j + 1):ROWS * (j + 2), :] = acc[o]

    def y_stage(k, view, odd, j):
        taps = [wy[k, i] for i in range(2 * RL + 1)]
        base = ROWS * (j + 1) - RL
        values = []
        for p in range(planes):
            value = None
            for o in range(2 * RL + 1):
                term = taps[o] * zb[p, base + o:base + o + ROWS, :]
                value = term if value is None else value + term
            value = f[0, j, p] * value if odd else moved[view, j, p] / value
            f[0 if odd else 1, j, p] = value
            values.append(value)
        pack_edges(values, 0 if odd else 1, j)

    def y_waits(view, odd, j, on):
        gone(0 if odd else 1, j, on)
        if not odd:
            dw = lax.rem(w + j // own, 2)
            r = j % own
            guarded(jnp.logical_or(away, dw > 0), lambda: bulk(view, r, dw).wait_recv())
            bulk(view, r, 2 + dw).wait_recv()

    def finish(j):
        for tc in range(2):
            far_copy, near_copy, local = back(j, tc)
            guarded(local, lambda: near_copy.start())
            guarded(jnp.logical_not(local), lambda: far_copy.start())

    for i in range(own):
        enter(i)
    for r in range(own):
        for u in range(PIECES):
            bulk_start(0, r, u)

    steps = 2 * chunks

    def one_view(view, carry):
        for i in range(steps):
            e, j = divmod(i, chunks)
            oy, jy = divmod((i - 2) % steps, chunks)
            r, u = divmod((i - 2) % steps, PIECES)
            arrive(e, j)
            if i >= 2:
                y_waits(view, oy, jy, None if oy else view > 0)
                x_stage(2 * view + e, e, j)
                y_stage(2 * view + oy, view, oy, jy)
                emit(1 - oy, jy, view < views - 1 if oy else None)
                if oy:
                    guarded(view == views - 1, lambda: finish(jy))
                bulk_start(view + 1, r, u, view < views - 1)
            else:
                x_stage(2 * view + e, e, j)

                def before():
                    y_waits(view - 1, 1, jy, None)
                    y_stage(2 * view - 1, view - 1, 1, jy)
                    emit(0, jy)
                    bulk_start(view, r, u)

                guarded(view > 0, before)
            z_stage(2 * view + e, j)
        return carry

    lax.fori_loop(0, views, one_view, 0)
    for jy in (chunks - 2, chunks - 1):
        y_waits(views - 1, 1, jy, None)
        y_stage(2 * views - 1, views - 1, 1, jy)
        finish(jy)

    for j in range(chunks):
        gone(1, j)
        for tc in range(2):
            far_copy, near_copy, local = back(j, tc)
            guarded(local, lambda: near_copy.wait())
            guarded(jnp.logical_not(local), lambda: far_copy.wait())
    for r in range(own):
        guarded(away, lambda: est_copy(r, 0).wait_send())
        for k in range(1, 4):
            est_copy(r, k).wait_send()

    def delivered(p, carry):
        for r in range(own):
            guarded(away, lambda: bulk(p, r, 0).wait_send())
            for k in range(1, 4):
                bulk(p, r, k).wait_send()
        return carry

    lax.fori_loop(0, views, delivered, 0)


def build_weights(views, psf_z, psf_y, psf_x, extents, order, wz, wy, xm, xe):
    def iota(shape, dim):
        return lax.broadcasted_iota(jnp.int32, shape, dim)

    x_which = iota((LANES, LANES), 0) - iota((LANES, LANES), 1) + RL
    r = iota((16, LANES), 0)
    e_which = jnp.where(r < 8, r - 8, r + (LANES - 8)) - iota((16, LANES), 1) + RL
    for p in range(views):
        view = order[p]
        tz = taps_of(psf_z, view, (extents[view, 0] - 1) // 2, RZ)
        ty = taps_of(psf_y, view, (extents[view, 1] - 1) // 2, RL)
        tx = taps_of(psf_x, view, (extents[view, 2] - 1) // 2, RL)
        for i in (2 * p, 2 * p + 1):
            for k in range(2 * RZ + 1):
                wz[i, k] = tz[k]
            for k in range(2 * RL + 1):
                wy[i, k] = ty[k]
            hi, lo = band(tx, x_which)
            for top in (0, LANES):
                xm[i, top:top + LANES, :LANES] = hi
                xm[i, top:top + LANES, LANES:] = lo
            hi, lo = band(tx, e_which)
            xe[i] = jnp.zeros(xe.shape[1:], xe.dtype)
            for top in (0, LANES):
                xe[i, top:top + 16, :LANES] = hi
                xe[i, top:top + 16, LANES:] = lo
            tz, ty, tx = tz[::-1], ty[::-1], tx[::-1]


def slabs(chain, estimate, measured, psf_z, psf_y, psf_x, extents, order):
    views, nz, ny, nx = measured.shape
    planes, rows = 2 * nz, 2 * ny
    chunks, own, blurs = rows // ROWS, ny // ROWS, 2 * views
    f32, bf16 = jnp.float32, jnp.bfloat16
    smem = pl.BlockSpec(memory_space=pltpu.SMEM)
    anywhere = pl.BlockSpec(memory_space=pl.ANY)
    dma = pltpu.SemaphoreType.DMA
    ways = len(WAYS)
    packed = planes * 8 // LANES
    return pl.pallas_call(
        functools.partial(wavefront_kernel, chain, nz, ny, views),
        out_shape=jax.ShapeDtypeStruct((nz, ny, nx), f32),
        in_specs=[anywhere] * 2 + [smem] * 5,
        out_specs=anywhere,
        scratch_shapes=[
            pltpu.VMEM((blurs, 2 * RZ + 1, ROWS, LANES), f32),
            pltpu.VMEM((blurs, 2 * RL + 1, ROWS, LANES), f32),
            pltpu.VMEM((blurs, 2 * LANES, 2 * LANES), bf16),
            pltpu.VMEM((blurs, 2 * LANES, 2 * LANES), bf16),
            pltpu.VMEM((2, chunks, planes, ROWS, LANES), f32),
            pltpu.VMEM((2, 2, chunks, RZ, ROWS, LANES), f32),
            pltpu.VMEM((2, planes + 2 * RZ, ROWS, LANES), f32),
            pltpu.VMEM((planes, rows + 2 * ROWS, LANES), f32),
            pltpu.VMEM((2, 2, chunks, packed, ROWS, LANES), f32),
            pltpu.VMEM((2, 2, chunks, packed + 2, ROWS, LANES), f32),
            pltpu.VMEM((views, nz, ny, nx), f32),
            pltpu.VMEM((views, nz, ny, nx), f32),
            pltpu.VMEM((views, chunks, planes, ROWS, LANES), f32),
            dma((ways, 2, chunks)), dma((ways, 2, chunks)),
            dma((own, 4)), dma((own, 4)),
            dma((views, own, 4)), dma((views, own, 4)),
            dma((own, 4)), dma((own, 4)),
            dma((own,)), dma((own,)), dma,
        ],
        compiler_params=pltpu.CompilerParams(collective_id=1, has_side_effects=True),
    )(estimate, measured, psf_z, psf_y, psf_x, extents, order)


def on_device(estimate, measured, psf_z, psf_y, psf_x, extents, order):
    n_z, n_y = lax.axis_size("gz"), lax.axis_size("gy")
    nz, ny, nx = estimate.shape
    fits = n_y == 2 and n_z % 4 == 0 and nx == 4 * LANES and nz == 16 and 2 * ny == 64
    if fits:
        return slabs(n_z // 2, estimate, measured, psf_z, psf_y, psf_x, extents, order)
    return general(estimate, measured, psf_z, psf_y, psf_x, extents, order)


def solution(mesh):
    return jax.shard_map(
        on_device,
        mesh=mesh,
        in_specs=(P("gz", "gy", None), P(None, "gz", "gy", None), P(), P(), P(), P(), P()),
        out_specs=P("gz", "gy", None),
        check_vma=False,
    )
```

time: 120 us -> 111 us (0.925)
  Pallas kernels: 117 us -> 109 us
    pallas_call x1, Pallas kernels: 117 us -> 109 us  [slabs(): pl.pallas_call(functools.partial(wavefront_kernel, chain, nz, ny, views),...]
where the time goes in v2:
time: 111 us
  Pallas kernels  109 us (98%)
  local copies, waits for them, and re-layouts  2.29 us (2%)
    pallas_call x1, Pallas kernels, slabs(): pl.pallas_call(functools.partial(wavefront_kernel, chain, nz, ny, views),...  109 us
    unnamed x1, local copies, waits for them, and re-layouts  2.29 us

profile of v2, /device:TPU:19, one launch (start us, length us, event | category | flops | bytes accessed | tf_op | source)
XLA Modules:
  0.0 111.0 jit_solution(15331262190272681393)
XLA Ops:
  0.0 108.7 %shard_map.73 = f32[16,32,512]{2,1,0:T(8,128)} custom-call(f32[16,32,512]{2,1,0:T(8,128)} %est.1, f32[4,16,32,512]{3,2,1,0:T(8,128)} %measured.1, f32[4,31]{1,0:T(4,128)} %psf_z.1, f32[4,15]{1,0:T(4,128)} %psf_y.1, f32[4,15]{1,0:T(4,128)} %psf_x.1, s32[4,3]{1,0:T(4,128)} %extents.1, s32[4]{0:T(128)} %order.1), custom_call_target="tpu_custom_call" | custom-call | tf_op jit(solution)/shard_map/pallas_call | solution.py:469
  108.7 2.3 %copy.9 = f32[16,32,512]{2,1,0:T(8,128)} copy(f32[16,32,512]{2,1,0:T(8,128)} %shard_map.73) | data formatting | bytes 2097152

commit v3 on v2

--- a/solution.py
+++ b/solution.py
@@ -111,7 +111,7 @@
 
 ROWS = 8
 PIECES = 4
-GROUPS = 2
+GROUPS = 1
 WAYS = [(1, -1), (-1, -1), (1, 1), (-1, 1), (0, -1), (0, 1), (1, 0), (-1, 0)]
 
 

time: 111 us -> 111 us (level)
  no operation moved by 1% of the time
where the time goes in v3:
time: 111 us
  Pallas kernels  109 us (98%)
  local copies, waits for them, and re-layouts  2.29 us (2%)
    pallas_call x1, Pallas kernels, slabs(): pl.pallas_call(functools.partial(wavefront_kernel, chain, nz, ny, views),...  109 us
    unnamed x1, local copies, waits for them, and re-layouts  2.29 us

profile of v3, /device:TPU:19, one launch (start us, length us, event | category | flops | bytes accessed | tf_op | source)
XLA Modules:
  0.0 111.3 jit_solution(5819370714136602225)
XLA Ops:
  0.0 109.0 %shard_map.73 = f32[16,32,512]{2,1,0:T(8,128)} custom-call(f32[16,32,512]{2,1,0:T(8,128)} %est.1, f32[4,16,32,512]{3,2,1,0:T(8,128)} %measured.1, f32[4,31]{1,0:T(4,128)} %psf_z.1, f32[4,15]{1,0:T(4,128)} %psf_y.1, f32[4,15]{1,0:T(4,128)} %psf_x.1, s32[4,3]{1,0:T(4,128)} %extents.1, s32[4]{0:T(128)} %order.1), custom_call_target="tpu_custom_call" | custom-call | tf_op jit(solution)/shard_map/pallas_call | solution.py:469
  109.0 2.3 %copy.9 = f32[16,32,512]{2,1,0:T(8,128)} copy(f32[16,32,512]{2,1,0:T(8,128)} %shard_map.73) | data formatting | bytes 2097152
